TPU v7x, 32 devices: a whole 2x2x4 slice. The times are simulated.
32 devices in a mesh: expert: 8 (over y, x, core), dp: 4 (over z).
Axes of the slice: x: 2, y: 2, z: 4, core: 2. Of those that a mesh axis runs over, the one named last changes fastest.
Arguments:
- out_grads: bfloat16 [4, 1024, 7168], P('dp', 'expert'), may hold values from -6 to 6
- expert_ids: int32 [4, 1024, 8], P('dp', 'expert'), may hold values from 0 to 63, all different within a row; in each aligned block of 128 rows (0 to 127, 128 to 255, ..., all dimensions but the last counted through in order) at most 24 rows name the same one
- gate_probs: float32 [4, 1024, 8], P('dp', 'expert'), may hold values from 0.05 to 0.5
- hidden_acts: bfloat16 [4, 64, 192, 2048], P('dp', 'expert'), may hold values from -6 to 6
- q_previous: bfloat16 [64, 32, 7168], P('expert'), may hold values from -0.0625 to 0.0625
Outputs:
- new_basis: float32 [64, 32, 2048], P('expert')
- q_update: float32 [64, 32, 7168], P('expert', None, 'dp')
Inputs may be any that keep to these rules, and one draw needn't show every extreme that they name: `expert_ids`: each row names 8 different experts; among the rows of one device no expert is named more than 24 times.
All inputs are finite; a program needn't handle non-finite values.
Results may differ from a plain program's by a relative error of at most 0.014.
Values may be sent and summed in bfloat16 or wider, within the bound.
A program may use at most 192 MiB of HBM per device.

v0:
```python
import math

import jax
import jax.numpy as jnp
from jax import lax
from jax.sharding import PartitionSpec as P


def slot_tables(route_ids, gate_values, num_experts, capacity):
    flat_ids = route_ids.reshape(-1)
    row_count = flat_ids.shape[0]
    top_k = route_ids.shape[-1]
    one_hot = (flat_ids[:, None] == jnp.arange(num_experts, dtype=jnp.int32)[None, :]).astype(
        jnp.int32
    )
    earlier = jnp.cumsum(one_hot, axis=0) - one_hot
    position = jnp.sum(earlier * one_hot, axis=1)
    slot_index = flat_ids * capacity + position
    token_of = (
        jnp.zeros((num_experts * capacity,), jnp.int32)
        .at[slot_index]
        .set(jnp.arange(row_count, dtype=jnp.int32) // top_k)
    )
    gate_of = (
        jnp.zeros((num_experts * capacity,), jnp.float32)
        .at[slot_index]
        .set(gate_values.reshape(-1))
    )
    return (token_of, gate_of)


def first_factor(arrived, q_part, hidden_part):
    mixed = jnp.einsum(
        "sjcd,jrd->jscr", arrived, q_part, preferred_element_type=jnp.float32
    ).astype(jnp.bfloat16)
    return jnp.einsum("jscr,jscf->jrf", mixed, hidden_part, preferred_element_type=jnp.float32)


def second_factor(arrived, projected):
    return jnp.einsum("jscr,sjcd->jrd", projected, arrived, preferred_element_type=jnp.float32)


def lower_inverse(gram):
    lower = jnp.linalg.cholesky(gram)
    identity = jnp.broadcast_to(jnp.eye(gram.shape[1], dtype=jnp.float32), gram.shape)
    return jax.vmap(lambda left, right: jax.scipy.linalg.solve_triangular(left, right, lower=True))(
        lower, identity
    )


def gram_of(values):
    return jnp.einsum("jrf,jsf->jrs", values, values, precision=lax.Precision.HIGHEST)


def apply_inverse(inverse, values):
    return jnp.einsum("jrs,jsf->jrf", inverse, values, precision=lax.Precision.HIGHEST)


def local(out_grads, expert_ids, gate_probs, hidden_acts, q_previous):
    n_expert = lax.axis_size("expert")
    local_count = hidden_acts.shape[1]
    slot_count = hidden_acts.shape[2]
    capacity = slot_count // n_expert
    width = out_grads.shape[2]
    token_of, gate_of = slot_tables(expert_ids[0], gate_probs[0], local_count * n_expert, capacity)
    picked = jnp.take(out_grads[0], token_of, axis=0)
    routed = (picked.astype(jnp.float32) * gate_of[:, None]).astype(jnp.bfloat16)
    routed = routed.reshape(n_expert, local_count, capacity, width)
    hidden_blocks = hidden_acts[0].reshape(local_count, n_expert, capacity, hidden_acts.shape[3])
    arrived = lax.all_to_all(routed, "expert", split_axis=0, concat_axis=0, tiled=True)
    factor = first_factor(arrived, q_previous, hidden_blocks)
    share = lax.psum_scatter(factor, "dp", scatter_dimension=2, tiled=True)
    gram = lax.psum(gram_of(share).astype(jnp.bfloat16), "dp").astype(jnp.float32)
    inverse = lower_inverse(gram)
    ortho = lax.all_gather(
        apply_inverse(inverse, share).astype(jnp.bfloat16), "dp", axis=2, tiled=True
    ).astype(jnp.float32)
    ortho_half = ortho.astype(jnp.bfloat16)
    projected = jnp.einsum(
        "jscf,jrf->jscr", hidden_blocks, ortho_half, preferred_element_type=jnp.float32
    ).astype(jnp.bfloat16)
    terms = second_factor(arrived, projected)
    q_update = lax.psum_scatter(
        terms.astype(jnp.bfloat16), "dp", scatter_dimension=2, tiled=True
    ).astype(jnp.float32)
    new_basis = ortho * math.sqrt(ortho.shape[2])
    return (new_basis, q_update)


def solution(mesh):
    return jax.shard_map(
        local,
        mesh=mesh,
        in_specs=(
            P("dp", "expert", None),
            P("dp", "expert", None),
            P("dp", "expert", None),
            P("dp", "expert", None, None),
            P("expert", None, None),
        ),
        out_specs=(P("expert", None, None), P("expert", None, "dp")),
        check_vma=False,
    )
```

profile of v0, /device:TPU:0, one launch (start us, length us, event | category | flops | bytes accessed | tf_op | source)
XLA Modules:
  0.0 552.8 jit_solution(5613829965889337958)
XLA Ops:
  7.2 0.0 copy-start
  7.2 0.0 reduce-scatter.3.cloned.1.call-start
  7.2 0.9 copy.32
  8.1 0.1 eq.30
  8.2 0.1 eq.26
  8.3 0.7 broadcast_multiply_fusion
  9.0 18.0 %reduce-window.6 = s32[64,8,128]{2,1,0:T(8,128)S(1)} reduce-window(s32[64,8,128]{2,1,0:T(8,128)S(1)} %fusion.25, s32[]{:T(128)} %constant.77.clone.1), window={size=1x1x128 pad=0_0x0_0x127_0}, to_apply=%region_0.0 | reduce-window | flops 8323072 | bytes 524292 | tf_op jit(solution)/shard_map/reduce-window
  27.1 0.1 slice.22
  27.2 0.1 copy.34
  27.4 0.1 copy.35
  27.5 0.1 broadcast_add_fusion
  27.6 0.1 copy.31
  27.7 0.1 mul.38
  27.8 0.1 fusion.24
  27.9 4.3 scatter_custom_fusion
  32.3 0.1 broadcast_in_dim.32
  32.4 0.8 copy.36
  33.1 0.1 reshape.99
  33.2 4.3 scatter_custom_fusion.1
  37.6 0.1 mul.40
  37.7 16.4 %gather_fusion = bf16[1536,7168]{1,0:T(8,128)(2,1)} fusion(bf16[128,7168]{1,0:T(8,128)(2,1)S(1)} %bitcast.63, s32[2048]{0:T(1024)S(1)} %pad_clamp_fusion), kind=kCustom, calls=%fused_computation | custom fusion | bytes 44046336 | tf_op jit(solution)/shard_map/jit(_take)/gather | solution.py:66
  54.1 10.0 %multiply_convert_fusion = bf16[8,8,24,7168]{3,2,1,0:T(8,128)(2,1)S(1)} fusion(f32[8,8,24]{2,1,0:T(8,128)S(1)} %mul.40, bf16[8,8,24,7168]{3,2,1,0:T(8,128)(2,1)} %bitcast.64, pred[8,8,24]{2,1,0:T(8,128)(4,1)S(1)} %broadcast_in_dim.32), kind=kLoop, calls=%fused_computation.3 | loop fusion | flops 44040192 | bytes 44047872 | tf_op jit(solution)/shard_map/convert_element_type | solution.py:67
  64.1 245.1 %all_to_all.5 = bf16[8,8,24,7168]{3,2,1,0:T(8,128)(2,1)} all-to-all(bf16[8,8,24,7168]{3,2,1,0:T(8,128)(2,1)S(1)} %multiply_convert_fusion), channel_id=1, replica_groups=mesh['expert'=8,'dp'=4] {'expert'}, dimensions={0} | all-to-all | bytes 44040192 | tf_op jit(solution)/shard_map/all_to_all | solution.py:70
  309.2 14.6 %convolution_bitcast_fusion = f32[8,32,2048]{2,1,0:T(8,128)} fusion(bf16[8,8,24,2048]{3,2,1,0:T(8,128)(2,1)} %bitcast.70, bf16[8,32,7168]{2,1,0:T(8,128)(2,1)} %param.9, bf16[8,8,24,7168]{3,2,1,0:T(8,128)(2,1)} %all_to_all.5), kind=kOutput, calls=%fused_computation.11 | convolution fusion | flops 906018816 | bytes 34078720 | tf_op jit(solution)/shard_map/jscr,jscf->jrf/dot_general | solution.py:36
  323.8 0.0 reduce-scatter.3.cloned.1.call-update
  323.8 0.0 all-gather.2.cloned.1.call-start
  323.9 43.4 %reduce-scatter.3.cloned.1.call-done = f32[8,32,512]{2,1,0:T(8,128)} async-done(((f32[8,32,2048]{2,1,0:T(8,128)}), f32[8,32,512]{2,1,0:T(8,128)}) %reduce-scatter.3.cloned.1.call-update) | async-done | bytes 524304 | tf_op jit(solution)/shard_map/reduce_scatter | solution.py:72
  367.4 1.8 convolution_convert_fusion.2
  369.2 18.1 %psum.7 = bf16[8,32,32]{1,2,0:T(8,128)(2,1)S(1)} all-reduce(bf16[8,32,32]{1,2,0:T(8,128)(2,1)S(1)} %convolution_convert_fusion.2), channel_id=1, replica_groups=mesh['expert'=8,'dp'=4] {'dp'}, use_global_device_ids=true, to_apply=%region_6.7 | all-reduce | flops 8192 | bytes 32768 | tf_op jit(solution)/shard_map/psum | solution.py:73
  387.3 0.1 copy.39
  387.4 23.4 %custom-call.8 = f32[8,32,32]{2,1,0:T(8,128)S(1)} custom-call(f32[8,32,32]{2,1,0:T(8,128)S(1)} %fusion.28), custom_call_target="Cholesky" | custom-call | tf_op jit(solution)/shard_map/jit(cholesky)/cholesky | solution.py:44
  410.9 0.1 compare_reduce_fusion
  411.0 0.1 select_bitcast_fusion
  411.1 19.7 %custom-call.9 = f32[8,1,32,32]{2,3,1,0:T(8,128)S(1)} custom-call(f32[8,1,32,32]{3,2,1,0:T(8,128)S(1)} %select_bitcast_fusion), custom_call_target="InvertDiagBlocksLowerTriangular" | custom-call | tf_op jit(solution)/shard_map/vmap(jit(_solve_triangular))/triangular_solve | solution.py:46
  430.8 0.4 fusion.26
  431.2 2.3 convolution_convert_fusion.1
  433.5 0.0 all-gather.2.cloned.1.call-update
  433.6 0.2 reduce-scatter.5.cloned.1.call-start
  433.8 26.0 %all-gather.2.cloned.1.call-done = bf16[8,32,2048]{2,1,0:T(8,128)(2,1)} async-done(((bf16[8,32,512]{2,1,0:T(8,128)(2,1)}), bf16[8,32,2048]{2,1,0:T(8,128)(2,1)}) %all-gather.2.cloned.1.call-update) | async-done | bytes 1048592 | tf_op jit(solution)/shard_map/all_gather | solution.py:75
  459.8 4.9 fusion.16
  464.7 0.0 copy-start.2
  464.7 0.0 copy-start.1
  464.7 10.9 %fusion.7 = bf16[8,32,7168]{2,1,0:T(8,128)(2,1)} fusion(bf16[8,8,24,32]{3,2,1,0:T(8,128)(2,1)S(1)} %fusion.16, bf16[8,8,24,7168]{3,2,1,0:T(8,128)(2,1)} %all_to_all.5), kind=kOutput, calls=%fused_computation.9 | convolution fusion | flops 706478080 | bytes 25788416 | tf_op jit(solution)/shard_map/jscr,sjcd->jrd/dot_general | solution.py:40
  475.6 0.0 reduce-scatter.5.cloned.1.call-update
  475.6 0.0 copy-done.2
  475.6 1.6 convert_multiply_fusion
  477.2 66.5 %reduce-scatter.5.cloned.1.call-done = bf16[8,32,1792]{2,1,0:T(8,128)(2,1)} async-done(((bf16[8,32,7168]{2,1,0:T(8,128)(2,1)}), bf16[8,32,1792]{2,1,0:T(8,128)(2,1)}) %reduce-scatter.5.cloned.1.call-update) | async-done | bytes 917520 | tf_op jit(solution)/shard_map/reduce_scatter | solution.py:83
  543.7 2.6 convert_element_type.59
  (15 shorter events, 0.2 us)
Async XLA Ops:
  7.2 30.5 %copy-start = (bf16[1,128,7168]{2,1,0:T(8,128)(2,1)S(1)}, bf16[1,128,7168]{2,1,0:T(8,128)(2,1)}, u32[]{:S(2)}) copy-start(bf16[1,128,7168]{2,1,0:T(8,128)(2,1)} %param.5) | copy-start | bytes 5505028
  7.2 360.2 %reduce-scatter.3.cloned.1.call-start = ((), (), s32[]{:S(2)}) async-start(), calls=%async_computation.3 | async-start | bytes 2621440 | tf_op jit(solution)/shard_map/reduce_scatter | solution.py:72
  323.8 135.9 %all-gather.2.cloned.1.call-start = ((), (), s32[]{:S(2)}) async-start(), calls=%async_computation.4 | async-start | bytes 1310720 | tf_op jit(solution)/shard_map/all_gather | solution.py:75
  433.6 110.2 %reduce-scatter.5.cloned.1.call-start = ((), (), s32[]{:S(2)}) async-start(), calls=%async_computation.5 | async-start | bytes 4587520 | tf_op jit(solution)/shard_map/reduce_scatter | solution.py:83
  464.7 10.9 %copy-start.2 = (bf16[8,32,2048]{2,1,0:T(8,128)(2,1)S(1)}, bf16[8,32,2048]{2,1,0:T(8,128)(2,1)}, u32[]{:S(2)}) copy-start(bf16[8,32,2048]{2,1,0:T(8,128)(2,1)} %all-gather.2.cloned.1.call-done) | copy-start | bytes 3145732
  464.7 81.6 %copy-start.1 = (bf16[1,128,7168]{2,1,0:T(8,128)(2,1)S(1)}, bf16[1,128,7168]{2,1,0:T(8,128)(2,1)}, u32[]{:S(2)}) copy-start(bf16[1,128,7168]{2,1,0:T(8,128)(2,1)} %param.5) | copy-start | bytes 5505028
Sparse Core Ops, SparseCore 0:
  324.0 43.3 reduce-scatter.2
  433.7 26.0 all-gather.1
  475.8 67.9 reduce-scatter.4
where the time goes:
time: 553 us
  blocking collectives  263 us (48%)
  waiting for transfers between devices  136 us (25%)
  other arithmetic  76.5 us (14%)
  matrix products  34.9 us (6%)
  local copies, waits for them, and re-layouts  27.9 us (5%)
  between operations  14 us (3%)
    all_to_all x1, blocking collectives, local(): lax.all_to_all(routed, 'expert', split_axis=0, concat_axis=0, tiled=True)  245 us
    reduce_scatter x1, waiting for transfers between devices, local(): lax.psum_scatter(terms.astype(jnp.bfloat16), 'dp', scatter_dimension=2, t...  66.5 us
    reduce_scatter x1, waiting for transfers between devices, local(): share = lax.psum_scatter(factor, 'dp', scatter_dimension=2, tiled=True)  43.4 us
    all_gather x1, waiting for transfers between devices, local(): lax.all_gather(apply_inverse(inverse, share).astype(jnp.bfloat16), 'dp',...  26 us
    another operation x4, other arithmetic, lower_inverse(): lower = jnp.linalg.cholesky(gram)  23.6 us
    another operation x3, other arithmetic, lower_inverse(): jax.scipy.linalg.solve_triangular(left, right, lower=True)  19.8 us
    another operation x3, other arithmetic  18.2 us
    psum x1, blocking collectives, local(): lax.psum(gram_of(share).astype(jnp.bfloat16), 'dp').astype(jnp.float32)  18.1 us
  transfers between devices with their start and end apart: 3, of which 3 were waited for; matrix products, arithmetic and copies ran while one was open for 0% of the time, Pallas kernels for 0%

commit v1 on v0

v1 whole, which is shorter than its diff:
```python
import functools
import math

import jax
import jax.numpy as jnp
from jax import lax
from jax.experimental import pallas as pl
from jax.experimental.pallas import tpu as pltpu
from jax.sharding import PartitionSpec as P

F32, BF16 = jnp.float32, jnp.bfloat16


def inverse_kernel(factor_ref, ortho_ref):
    count, rank, _ = factor_ref.shape
    rows = lax.broadcasted_iota(jnp.int32, (rank, 2 * rank), 0)
    cols = lax.broadcasted_iota(jnp.int32, (rank, 2 * rank), 1)
    eye = (cols == rows + rank).astype(F32)
    tables = []
    for j in range(count):
        value = factor_ref[j]
        doubled = jnp.concatenate([value, jnp.zeros_like(value)], axis=0)
        gram = lax.dot_general(
            value, doubled, (((1,), (1,)), ((), ())),
            precision=lax.Precision.HIGHEST, preferred_element_type=F32,
        )
        tables.append(gram + eye)
    for k in range(rank):
        for j in range(count):
            table = tables[j]
            row = table[k : k + 1, :]
            pivot = lax.rsqrt(row[:, k : k + 1])
            scaled = row * pivot
            column = table[:, k : k + 1] * pivot
            table = jnp.where(rows > k, table - column * scaled, table)
            tables[j] = jnp.where(rows == k, scaled, table)
    for j in range(count):
        ortho_ref[j] = jnp.dot(
            tables[j][:, rank:], factor_ref[j],
            precision=lax.Precision.HIGHEST, preferred_element_type=F32,
        ).astype(ortho_ref.dtype)


def orthonormal(factor):
    return pl.pallas_call(
        inverse_kernel,
        out_shape=jax.ShapeDtypeStruct(factor.shape, BF16),
        name="orthonormal",
    )(factor)


def local(out_grads, expert_ids, gate_probs, hidden_acts, q_previous):
    n_expert = lax.axis_size("expert")
    experts, slots, units = hidden_acts.shape[1:]
    capacity = slots // n_expert
    tokens, width = out_grads.shape[1:]
    rank = q_previous.shape[1]
    first = lax.axis_index("expert") * experts

    route = jnp.concatenate([expert_ids[0].astype(F32), gate_probs[0]], axis=1)
    route = lax.all_gather(route, "expert", axis=0)
    grads = lax.all_gather(out_grads[0], "expert", axis=0)
    top = expert_ids.shape[2]
    mine = (first + jnp.arange(experts)).astype(F32)
    hit = route[:, :, :top, None] == mine
    gate = jnp.sum(jnp.where(hit, route[:, :, top:, None], 0.0), axis=2)
    chosen = jnp.any(hit, axis=2)
    earlier = (jnp.arange(tokens)[:, None] > jnp.arange(tokens)[None, :]).astype(BF16)
    place = jnp.einsum("ut,btj->buj", earlier, chosen.astype(BF16), preferred_element_type=F32)
    place = jnp.where(chosen, place, -1.0).transpose(2, 0, 1)
    pick = (place[:, :, None, :] == jnp.arange(capacity, dtype=F32)[:, None]).astype(BF16)

    mixed = jnp.einsum("btd,jrd->btjr", grads, q_previous, preferred_element_type=F32)
    mixed = (mixed * gate[..., None]).astype(BF16)
    mixed = jnp.einsum("jbct,btjr->jbcr", pick, mixed, preferred_element_type=F32).astype(BF16)
    hidden = hidden_acts[0]
    factor = jnp.einsum(
        "jsr,jsf->jrf", mixed.reshape(experts, slots, rank), hidden, preferred_element_type=F32
    )
    share = lax.psum_scatter(factor, "dp", scatter_dimension=0, tiled=True)
    ortho = lax.all_gather(orthonormal(share), "dp", axis=0, tiled=True)
    projected = jnp.einsum("jsf,jrf->jsr", hidden, ortho, preferred_element_type=F32).astype(BF16)
    spread = jnp.einsum(
        "jbct,jbcr->btjr",
        pick,
        projected.reshape(experts, n_expert, capacity, rank),
        preferred_element_type=F32,
    )
    spread = (spread * gate[..., None]).astype(BF16)
    terms = jnp.einsum("btjr,btd->jrd", spread, grads, preferred_element_type=F32)
    q_update = lax.psum_scatter(
        terms.astype(BF16), "dp", scatter_dimension=2, tiled=True
    ).astype(F32)
    new_basis = ortho.astype(F32) * math.sqrt(units)
    return (new_basis, q_update)


def solution(mesh):
    return jax.shard_map(
        local,
        mesh=mesh,
        in_specs=(
            P("dp", "expert", None),
            P("dp", "expert", None),
            P("dp", "expert", None),
            P("dp", "expert", None, None),
            P("expert", None, None),
        ),
        out_specs=(P("expert", None, None), P("expert", None, "dp")),
        check_vma=False,
    )
```

time: 553 us -> 277 us (0.50)
  blocking collectives: 263 us -> 10.6 us
  waiting for transfers between devices: 136 us -> 211 us
  other arithmetic: 76.5 us -> 5.71 us
  local copies, waits for them, and re-layouts: 27.9 us -> 0.31 us
  matrix products: 34.9 us -> 28.6 us
  Pallas kernels: 0 us -> 5.72 us
    all_to_all x1 -> x0, blocking collectives: 245 us -> none  [local(): lax.all_to_all(routed, 'expert', split_axis=0, concat_axis=0, tiled=True)]
    all_gather x1 -> x2, waiting for transfers between devices: 26 us -> 100 us  [the longest x1 73.1 us: local(): grads = lax.all_gather(out_grads[0], 'expert', axis=0)]
    another operation x10 -> x0, other arithmetic: 61.6 us -> none  [the longest x4 23.6 us: lower_inverse(): lower = jnp.linalg.cholesky(gram)]
    psum x1 -> x0, blocking collectives: 18.1 us -> none  [local(): lax.psum(gram_of(share).astype(jnp.bfloat16), 'dp').astype(jnp.float32)]
    gather x1 -> x0, local copies, waits for them, and re-layouts: 16.4 us -> none  [local(): picked = jnp.take(out_grads[0], token_of, axis=0)]
    all_gather x0 -> x1, blocking collectives: none -> 10.6 us  [local(): route = lax.all_gather(route, 'expert', axis=0)]
    convert_element_type x4 -> x3, other arithmetic: 12.5 us -> 3.25 us  [the longest x1 2.56 us: local(): q_update = lax.psum_scatter(terms.astype(BF16), 'dp', scatter_dimension=2...]
    scatter x2 -> x0, local copies, waits for them, and re-layouts: 8.63 us -> none  [the longest x1 4.32 us: slot_tables(): token_of = jnp.zeros((num_experts * capacity,), jnp.int32).at[slot_index]...]
  transfers between devices with their start and end apart: 3 -> 4, of which waited for: 3 -> 4; matrix products, arithmetic and copies ran while one was open for 0% -> 1% of each run, Pallas kernels for 0% -> 0%
where the time goes in v1:
time: 277 us; the launch traced here: 276 us
  waiting for transfers between devices  211 us (76%)
  matrix products  28.6 us (10%)
  between operations  13.9 us (5%)
  blocking collectives  10.6 us (4%)
  Pallas kernels  5.72 us (2%)
  other arithmetic  5.71 us (2%)
    all_gather x1, waiting for transfers between devices, local(): grads = lax.all_gather(out_grads[0], 'expert', axis=0)  73.1 us
    reduce_scatter x1, waiting for transfers between devices, local(): lax.psum_scatter(terms.astype(BF16), 'dp', scatter_dimension=2, tiled=True)  66.5 us
    reduce_scatter x1, waiting for transfers between devices, local(): share = lax.psum_scatter(factor, 'dp', scatter_dimension=0, tiled=True)  43.7 us
    all_gather x1, waiting for transfers between devices, local(): ortho = lax.all_gather(orthonormal(share), 'dp', axis=0, tiled=True)  27.3 us
    all_gather x1, blocking collectives, local(): route = lax.all_gather(route, 'expert', axis=0)  10.6 us
    dot_general x1, matrix products, local(): jnp.einsum('btjr,btd->jrd', spread, grads, preferred_element_type=F32)  9.16 us
    dot_general x1, matrix products, local(): jnp.einsum('btd,jrd->btjr', grads, q_previous, preferred_element_type=F32)  8.34 us
    pallas_call x1, Pallas kernels, orthonormal(): pl.pallas_call(inverse_kernel, out_shape=jax.ShapeDtypeStruct(factor.shap...  5.72 us
  transfers between devices with their start and end apart: 4, of which 4 were waited for; matrix products, arithmetic and copies ran while one was open for 1% of the time, Pallas kernels for 0%

profile of v1, /device:TPU:0, one launch (start us, length us, event | category | flops | bytes accessed | tf_op | source)
XLA Modules:
  0.0 276.3 jit_solution(4871470031745781381)
XLA Ops:
  7.2 0.0 all-gather.4.cloned.1.call-start
  7.2 0.7 all-gather.4.cloned.1.call-update
  7.9 0.0 reduce-scatter.3.cloned.1.call-start
  7.9 0.7 convert_bitcast_fusion
  8.6 0.7 pad_maximum_fusion
  9.3 10.6 %all-gather = f32[1024,16]{0,1:T(8,128)S(1)} all-gather(f32[128,16]{0,1:T(8,128)S(1)} %pad_maximum_fusion), channel_id=2, replica_groups=mesh['expert'=8,'dp'=4] {'expert'}, dimensions={0}, use_global_device_ids=true | all-gather | bytes 73728 | tf_op jit(solution)/shard_map/all_gather | solution.py:61
  19.9 0.1 compare_reduce_fusion
  20.1 0.1 fusion.33
  20.2 0.1 fusion.38
  20.4 73.1 %all-gather.4.cloned.1.call-done = bf16[8,128,7168]{2,1,0:T(8,128)(2,1)} async-done(((bf16[1,128,7168]{2,1,0:T(8,128)(2,1)}), bf16[8,128,7168]{2,1,0:T(8,128)(2,1)}) %all-gather.4.cloned.1.call-update) | async-done | bytes 14680080 | tf_op jit(solution)/shard_map/all_gather | solution.py:62
  93.5 8.3 %fusion.22 = bf16[8,128,8,32]{1,3,0,2:T(8,128)(2,1)S(1)} fusion(bf16[8,32,7168]{2,1,0:T(8,128)(2,1)} %param.9, bf16[8,128,7168]{2,1,0:T(8,128)(2,1)} %all-gather.4.cloned.1.call-done, f32[8,128,8]{1,0,2:T(8,128)S(1)} %copy.23), kind=kOutput, calls=%fused_computation.16 | convolution fusion | flops 3758620672 | bytes 18907136 | tf_op jit(solution)/shard_map/btd,jrd->btjr/dot_general | solution.py:73
  101.8 0.4 convolution_convert_fusion
  102.2 5.4 %fusion.12 = f32[8,32,2048]{2,1,0:T(8,128)} fusion(bf16[8,192,32]{2,1,0:T(8,128)(2,1)S(1)} %bitcast.69, bf16[1,8,192,2048]{3,2,1,0:T(8,128)(2,1)} %param.8), kind=kOutput, calls=%fused_computation.8 | convolution fusion | flops 201326592 | bytes 8486912 | tf_op jit(solution)/shard_map/jsr,jsf->jrf/dot_general | solution.py:77
  107.6 0.0 reduce-scatter.3.cloned.1.call-update
  107.7 0.0 all-gather.6.cloned.1.call-start
  107.7 43.7 %reduce-scatter.3.cloned.1.call-done.factor_ref = f32[2,32,2048]{2,1,0:T(8,128)} async-done(((f32[8,32,2048]{2,1,0:T(8,128)}), f32[2,32,2048]{2,1,0:T(8,128)}) %reduce-scatter.3.cloned.1.call-update) | async-done | bytes 524304 | tf_op jit(solution)/shard_map/reduce_scatter | solution.py:80
  151.5 5.7 %orthonormal.1 = bf16[2,32,2048]{2,1,0:T(8,128)(2,1)} custom-call(f32[2,32,2048]{2,1,0:T(8,128)} %reduce-scatter.3.cloned.1.call-done.factor_ref), custom_call_target="tpu_custom_call" | custom-call | tf_op jit(solution)/shard_map/orthonormal/pallas_call | solution.py:45
  157.2 0.0 all-gather.6.cloned.1.call-update
  157.2 0.0 reduce-scatter.5.cloned.1.call-start
  157.3 27.3 %all-gather.6.cloned.1.call-done = bf16[8,32,2048]{2,1,0:T(8,128)(2,1)} async-done(((bf16[2,32,2048]{2,1,0:T(8,128)(2,1)}), bf16[8,32,2048]{2,1,0:T(8,128)(2,1)}) %all-gather.6.cloned.1.call-update) | async-done | bytes 1048592 | tf_op jit(solution)/shard_map/all_gather | solution.py:81
  184.5 5.2 %fusion.30 = bf16[8,192,32]{1,2,0:T(8,128)(2,1)S(1)} fusion(bf16[8,32,2048]{2,1,0:T(8,128)(2,1)} %all-gather.6.cloned.1.call-done, bf16[1,8,192,2048]{3,2,1,0:T(8,128)(2,1)} %param.8), kind=kOutput, calls=%fused_computation.19 | convolution fusion | flops 201375744 | bytes 7438336 | tf_op jit(solution)/shard_map/jsf,jrf->jsr/dot_general | solution.py:82
  189.7 0.2 copy.29
  189.9 0.0 copy-start
  189.9 9.2 %fusion.7 = bf16[8,32,7168]{2,1,0:T(8,128)(2,1)} fusion(bf16[8,128,7168]{2,1,0:T(8,128)(2,1)} %all-gather.4.cloned.1.call-done, bf16[8,8,24,32]{3,2,1,0:T(8,128)(2,1)S(1)} %bitcast.70, f32[8,128,8]{1,0,2:T(8,128)S(1)} %copy.23, f32[8,8,128]{2,1,0:T(8,128)S(1)} %copy.21), kind=kOutput, calls=%fused_computation.5 | convolution fusion | flops 3773235200 | bytes 18513920 | tf_op jit(solution)/shard_map/btjr,btd->jrd/dot_general | solution.py:90
  199.1 0.0 reduce-scatter.5.cloned.1.call-update
  199.1 0.0 copy-done
  199.1 1.6 convert_multiply_fusion
  200.7 66.5 %reduce-scatter.5.cloned.1.call-done = bf16[8,32,1792]{2,1,0:T(8,128)(2,1)} async-done(((bf16[8,32,7168]{2,1,0:T(8,128)(2,1)}), bf16[8,32,1792]{2,1,0:T(8,128)(2,1)}) %reduce-scatter.5.cloned.1.call-update) | async-done | bytes 917520 | tf_op jit(solution)/shard_map/reduce_scatter | solution.py:91
  267.2 2.6 convert_element_type.50
  (7 shorter events, 0.1 us)
Async XLA Ops:
  7.2 86.3 %all-gather.4.cloned.1.call-start = ((), (), s32[]{:S(2)}) async-start(), calls=%async_computation.2 | async-start | bytes 16515072 | tf_op jit(solution)/shard_map/all_gather | solution.py:62
  7.9 143.6 %reduce-scatter.3.cloned.1.call-start = ((), (), s32[]{:S(2)}) async-start(), calls=%async_computation.3 | async-start | bytes 2621440 | tf_op jit(solution)/shard_map/reduce_scatter | solution.py:80
  107.7 76.9 %all-gather.6.cloned.1.call-start = ((), (), s32[]{:S(2)}) async-start(), calls=%async_computation.4 | async-start | bytes 1310720 | tf_op jit(solution)/shard_map/all_gather | solution.py:81
  157.2 110.0 %reduce-scatter.5.cloned.1.call-start = ((), (), s32[]{:S(2)}) async-start(), calls=%async_computation.5 | async-start | bytes 4587520 | tf_op jit(solution)/shard_map/reduce_scatter | solution.py:91
  189.9 9.2 %copy-start = (bf16[8,32,2048]{2,1,0:T(8,128)(2,1)S(1)}, bf16[8,32,2048]{2,1,0:T(8,128)(2,1)}, u32[]{:S(2)}) copy-start(bf16[8,32,2048]{2,1,0:T(8,128)(2,1)} %all-gather.6.cloned.1.call-done) | copy-start | bytes 3145732
Sparse Core Ops, SparseCore 0:
  9.9 83.5 all-gather.3
  107.8 43.6 reduce-scatter.2
  157.3 27.1 all-gather.5
  199.3 67.9 reduce-scatter.4

commit v2 on v1

v2 whole, which is shorter than its diff:
```python
import functools
import math

import jax
import jax.numpy as jnp
from jax import lax
from jax.experimental import pallas as pl
from jax.experimental.pallas import tpu as pltpu
from jax.sharding import PartitionSpec as P

F32, BF16 = jnp.float32, jnp.bfloat16


MESH = pl.DeviceIdType.MESH


def orthonormal(value):
    rank = value[0].shape[0]
    rows = lax.broadcasted_iota(jnp.int32, (rank, 2 * rank), 0)
    cols = lax.broadcasted_iota(jnp.int32, (rank, 2 * rank), 1)
    eye = (cols == rows + rank).astype(F32)
    tables = []
    for one in value:
        doubled = jnp.concatenate([one, jnp.zeros_like(one)], axis=0)
        gram = lax.dot_general(
            one, doubled, (((1,), (1,)), ((), ())),
            precision=lax.Precision.HIGHEST, preferred_element_type=F32,
        )
        tables.append(gram + eye)
    for k in range(rank):
        for j, table in enumerate(tables):
            row = table[k : k + 1, :]
            pivot = lax.rsqrt(row[:, k : k + 1])
            scaled = row * pivot
            column = table[:, k : k + 1] * pivot
            table = jnp.where(rows > k, table - column * scaled, table)
            tables[j] = jnp.where(rows == k, scaled, table)
    return [
        jnp.dot(
            table[:, rank:], one, precision=lax.Precision.HIGHEST, preferred_element_type=F32
        )
        for table, one in zip(tables, value)
    ]


def factor_kernel(
    n, part_ref, hidden_ref, ortho_ref, proj_ref,
    hidden, got_part, fact, got_fact, load_sem, send_sem, recv_sem,
):
    me = lax.axis_index("dp")
    experts = hidden.shape[0]
    per = experts // n
    peers = [lax.rem(me + offset, n) for offset in range(1, n)]
    loads = []
    for j in range(experts):
        load = pltpu.make_async_copy(hidden_ref.at[j], hidden.at[j], load_sem.at[j])
        load.start()
        loads.append(load)
    barrier = pltpu.get_barrier_semaphore()
    for peer in peers:
        pl.semaphore_signal(barrier, inc=1, device_id={"dp": peer}, device_id_type=MESH)
    pl.semaphore_wait(barrier, n - 1)

    def push(phase, offset, source, target):
        copy = pltpu.make_async_remote_copy(
            src_ref=source,
            dst_ref=target,
            send_sem=send_sem.at[phase, offset],
            recv_sem=recv_sem.at[phase, offset],
            device_id={"dp": peers[offset]},
            device_id_type=MESH,
        )
        copy.start()
        return copy

    sent = [push(0, o, part_ref.at[peers[o]], got_part.at[o]) for o in range(n - 1)]
    for copy in sent:
        copy.wait()
    mixed = part_ref[me].astype(F32)
    for o in range(n - 1):
        mixed = mixed + got_part[o].astype(F32)
    mixed = mixed.astype(BF16)
    for load in loads:
        load.wait()
    rank = mixed.shape[1]
    for j in range(experts):
        fact[j] = jnp.dot(mixed[j], hidden[j], preferred_element_type=F32).astype(BF16)
    sent = [
        push(1, o, fact.at[pl.ds(peers[o] * per, per)], got_fact.at[o]) for o in range(n - 1)
    ]
    for copy in sent:
        copy.wait()
    share = []
    for i in range(per):
        total = fact[me * per + i].astype(F32)
        for o in range(n - 1):
            total = total + got_fact[o, i].astype(F32)
        share.append(total)
    for i, value in enumerate(orthonormal(share)):
        ortho_ref[me * per + i] = value.astype(BF16)
    mine = ortho_ref.at[pl.ds(me * per, per)]
    sent = [push(2, o, mine, mine) for o in range(n - 1)]

    def project(group):
        for i in range(per):
            j = group * per + i
            proj_ref[me, j] = lax.dot_general(
                ortho_ref[j], hidden[j], (((1,), (1,)), ((), ())), preferred_element_type=F32
            ).astype(BF16)

    project(me)
    for o in range(n - 1):
        sent[o].wait()
        project(lax.rem(me + n - 1 - o, n))
    sent = [push(3, o, proj_ref.at[me], proj_ref.at[me]) for o in range(n - 1)]
    for copy in sent:
        copy.wait()


def factors(part, hidden, n):
    experts, slots, units = hidden.shape
    rank = part.shape[2]
    per = experts // n
    vmem = pl.BlockSpec(memory_space=pltpu.VMEM)
    return pl.pallas_call(
        functools.partial(factor_kernel, n),
        out_shape=(
            jax.ShapeDtypeStruct((experts, rank, units), BF16),
            jax.ShapeDtypeStruct((n, experts, rank, slots), BF16),
        ),
        in_specs=[vmem, pl.BlockSpec(memory_space=pl.ANY)],
        out_specs=(vmem, vmem),
        scratch_shapes=[
            pltpu.VMEM((experts, slots, units), BF16),
            pltpu.VMEM((n - 1, experts, rank, slots), BF16),
            pltpu.VMEM((experts, rank, units), BF16),
            pltpu.VMEM((n - 1, per, rank, units), BF16),
            pltpu.SemaphoreType.DMA((experts,)),
            pltpu.SemaphoreType.DMA((4, n - 1)),
            pltpu.SemaphoreType.DMA((4, n - 1)),
        ],
        compiler_params=pltpu.CompilerParams(
            collective_id=0, has_side_effects=True, vmem_limit_bytes=40 * 2**20
        ),
        name="factors",
    )(part, hidden)


def gathered(grads):
    n_dp = lax.axis_size("dp")
    tokens, width = grads.shape
    split = grads.reshape(tokens, n_dp, width // n_dp).transpose(1, 0, 2)
    split = lax.all_to_all(split, "dp", split_axis=0, concat_axis=0, tiled=True)
    return lax.all_gather(split, "expert", axis=0)


def local(out_grads, expert_ids, gate_probs, hidden_acts, q_previous):
    n_expert = lax.axis_size("expert")
    n_dp = lax.axis_size("dp")
    experts, slots, units = hidden_acts.shape[1:]
    capacity = slots // n_expert
    tokens, width = out_grads.shape[1:]
    top = expert_ids.shape[2]
    rank = q_previous.shape[1]
    cols = width // n_dp
    first = lax.axis_index("expert") * experts

    route = jnp.concatenate([expert_ids[0].astype(F32), gate_probs[0]], axis=1)
    route = lax.all_gather(route, ("dp", "expert"), axis=0)
    route = route.reshape(n_dp, n_expert, tokens, 2 * top)
    grads = gathered(out_grads[0])
    mine = (first + jnp.arange(experts)).astype(F32)[:, None]
    ids = route[..., :top].transpose(3, 0, 1, 2)[:, :, :, None, :]
    weight = route[..., top:].transpose(3, 0, 1, 2)[:, :, :, None, :]
    hit = ids == mine
    gate = jnp.sum(jnp.where(hit, weight, 0.0), axis=0)
    chosen = jnp.any(hit, axis=0)
    earlier = (jnp.arange(tokens)[:, None] < jnp.arange(tokens)[None, :]).astype(BF16)
    place = jnp.einsum("pbjt,tu->pbju", chosen.astype(BF16), earlier, preferred_element_type=F32)
    place = jnp.where(chosen, place, -1.0)
    pick = (place[:, :, :, None, :] == jnp.arange(capacity, dtype=F32)[:, None]).astype(BF16)

    q_part = lax.dynamic_slice_in_dim(q_previous, lax.axis_index("dp") * cols, cols, 2)
    mixed = jnp.einsum("jrd,bptd->jrbpt", q_part, grads, preferred_element_type=F32)
    scale = gate.transpose(2, 1, 0, 3)
    mixed = (mixed * scale[:, None]).astype(BF16)
    part = jnp.einsum("jrbpt,pbjct->pjrbc", mixed, pick, preferred_element_type=F32).astype(BF16)
    part = part.reshape(n_dp, experts, rank, slots)
    ortho, proj = factors(part, hidden_acts[0], n_dp)
    proj = proj.reshape(n_dp, experts, rank, n_expert, capacity)
    spread = jnp.einsum("pjrbc,pbjct->jrbpt", proj, pick, preferred_element_type=F32)
    spread = (spread * scale[:, None]).astype(BF16)
    q_update = jnp.einsum("jrbpt,bptd->jrd", spread, grads, preferred_element_type=F32)
    new_basis = ortho.astype(F32) * math.sqrt(units)
    return (new_basis, q_update)


def solution(mesh):
    return jax.shard_map(
        local,
        mesh=mesh,
        in_specs=(
            P("dp", "expert", None),
            P("dp", "expert", None),
            P("dp", "expert", None),
            P("dp", "expert", None, None),
            P("expert", None, None),
        ),
        out_specs=(P("expert", None, None), P("expert", None, "dp")),
        check_vma=False,
    )
```

time: 277 us -> 261 us (0.942)
  waiting for transfers between devices: 211 us -> 39.5 us
  blocking collectives: 10.6 us -> 90 us
  Pallas kernels: 5.72 us -> 81.4 us
  local copies, waits for them, and re-layouts: 0.31 us -> 13.5 us
  matrix products: 28.6 us -> 19 us
  other arithmetic: 5.71 us -> 1.98 us
    reduce_scatter x2 -> x0, waiting for transfers between devices: 110 us -> none  [the longest x1 66.5 us: local(): lax.psum_scatter(terms.astype(BF16), 'dp', scatter_dimension=2, tiled=True)]
    pallas_call x1, Pallas kernels: 5.72 us -> 81.4 us  [factors(): pl.pallas_call(functools.partial(factor_kernel, n), out_shape=(jax.ShapeD...]
    all_gather x2 -> x1, waiting for transfers between devices: 100 us -> 39.5 us  [gathered(): return lax.all_gather(split, 'expert', axis=0)]
    all_to_all x0 -> x1, blocking collectives: none -> 48.9 us  [gathered(): split = lax.all_to_all(split, 'dp', split_axis=0, concat_axis=0, tiled=True)]
    all_gather x1, blocking collectives: 10.6 us -> 41.1 us  [local(): route = lax.all_gather(route, ('dp', 'expert'), axis=0)]
    dot_general x6 -> x3, matrix products: 28.6 us -> 19 us  [the longest x1 10.2 us: local(): jnp.einsum('jrbpt,bptd->jrd', spread, grads, preferred_element_type=F32)]
    unnamed x5 -> x10, local copies, waits for them, and re-layouts: 0.03 us -> 7.5 us
    reshape x1 -> x2, local copies, waits for them, and re-layouts: 0.24 us -> 3.35 us  [the longest x1 2.59 us: local(): proj = proj.reshape(n_dp, experts, rank, n_expert, capacity)]
  transfers between devices with their start and end apart: 4 -> 1, of which waited for: 4 -> 1; matrix products, arithmetic and copies ran while one was open for 1% -> 0% of each run, Pallas kernels for 0% -> 0%
where the time goes in v2:
time: 261 us; the launch traced here: 260 us
  blocking collectives  90 us (34%)
  Pallas kernels  81.4 us (31%)
  waiting for transfers between devices  39.5 us (15%)
  matrix products  19 us (7%)
  between operations  14.2 us (5%)
  local copies, waits for them, and re-layouts  13.5 us (5%)
    pallas_call x1, Pallas kernels, factors(): pl.pallas_call(functools.partial(factor_kernel, n), out_shape=(jax.ShapeD...  81.4 us
    all_to_all x1, blocking collectives, gathered(): split = lax.all_to_all(split, 'dp', split_axis=0, concat_axis=0, tiled=True)  48.9 us
    all_gather x1, blocking collectives, local(): route = lax.all_gather(route, ('dp', 'expert'), axis=0)  41.1 us
    all_gather x1, waiting for transfers between devices, gathered(): return lax.all_gather(split, 'expert', axis=0)  39.5 us
    dot_general x1, matrix products, local(): jnp.einsum('jrbpt,bptd->jrd', spread, grads, preferred_element_type=F32)  10.2 us
    dot_general x1, matrix products, local(): jnp.einsum('jrbpt,pbjct->pjrbc', mixed, pick, preferred_element_type=F32)  8.57 us
    unnamed x10, local copies, waits for them, and re-layouts  7.5 us
  transfers between devices with their start and end apart: 1, of which 1 were waited for; matrix products, arithmetic and copies ran while one was open for 0% of the time, Pallas kernels for 0%

profile of v2, /device:TPU:0, one launch (start us, length us, event | category | flops | bytes accessed | tf_op | source)
XLA Modules:
  0.0 259.5 jit_solution(3411569115506470230)
XLA Ops:
  7.2 0.0 all-gather.4.cloned.1.call-start
  7.2 3.9 %copy.32 = bf16[1,128,7168]{1,2,0:T(8,128)(2,1)} copy(bf16[1,128,7168]{2,1,0:T(8,128)(2,1)} %param.5) | data formatting | bytes 3670016 | tf_op args[0]
  11.1 48.9 %all_to_all.5 = bf16[4,128,1792]{1,2,0:T(8,128)(2,1)S(1)} all-to-all(bf16[4,128,1792]{1,2,0:T(8,128)(2,1)} %bitcast.53), channel_id=1, replica_groups=mesh['expert'=8,'dp'=4] {'dp'}, dimensions={0} | all-to-all | bytes 3670016 | tf_op jit(solution)/shard_map/all_to_all | solution.py:153
  60.0 0.0 copy-start.2
  60.0 0.0 copy-start.3
  60.0 2.4 copy.33
  62.4 0.0 all-gather.4.cloned.1.call-update
  62.5 0.0 copy-done.2
  62.5 0.0 copy-done.3
  62.5 41.1 %all-gather = f32[4096,16]{0,1:T(8,128)S(1)} all-gather(f32[128,16]{0,1:T(8,128)S(1)} %pad_maximum_fusion), channel_id=2, replica_groups=mesh['expert'=8,'dp'=4] {'dp','expert'}, dimensions={0}, use_global_device_ids=true | all-gather | bytes 270336 | tf_op jit(solution)/shard_map/all_gather | solution.py:169
  103.6 0.1 copy.49
  103.7 0.2 fusion.18
  103.9 0.1 copy.39
  104.0 0.2 compare_reduce_fusion
  104.2 0.2 convolution_select_fusion
  104.4 0.1 copy.31
  104.4 39.5 %all-gather.4.cloned.1.call-done = bf16[32,128,1792]{2,1,0:T(8,128)(2,1)} async-done(((bf16[4,128,1792]{2,1,0:T(8,128)(2,1)}), bf16[32,128,1792]{2,1,0:T(8,128)(2,1)}) %all-gather.4.cloned.1.call-update) | async-done | bytes 14680080 | tf_op jit(solution)/shard_map/all_gather | solution.py:154
  143.9 8.6 %fusion.7 = bf16[4,8,8,24,32]{4,3,2,1,0:T(8,128)(2,1)S(1)} fusion(f32[8,8,4,128]{3,1,0,2:T(8,128)S(1)} %copy.35, bf16[8,4,128,1792,1]{3,2,1,0,4:T(8,128)(2,1)} %bitcast.60, bf16[8,32,7168]{2,1,0:T(8,128)(2,1)} %param.9, s32[]{:T(128)S(6)} %select_n.12, f32[4,8,8,128]{3,0,1,2:T(4,128)S(1)} %copy.31), kind=kOutput, calls=%fused_computation.12 | convolution fusion | flops 3811508224 | bytes 16252932 | tf_op jit(solution)/shard_map/jrbpt,pbjct->pjrbc/dot_general | solution.py:187
  152.5 0.8 copy.48.part_ref
  153.3 0.0 copy-start
  153.3 2.8 %copy-done = bf16[1,8,192,2048]{3,2,1,0:T(8,128)(2,1)S(1)} copy-done((bf16[1,8,192,2048]{3,2,1,0:T(8,128)(2,1)S(1)}, bf16[1,8,192,2048]{3,2,1,0:T(8,128)(2,1)}, u32[]{:S(2)}) %copy-start) | copy-done | bytes 6291480
  156.1 81.4 %factors.1 = (bf16[8,32,2048]{2,1,0:T(8,128)(2,1)S(1)}, bf16[4,8,32,192]{3,2,1,0:T(8,128)(2,1)S(1)}) custom-call(bf16[4,8,32,192]{3,2,1,0:T(8,128)(2,1)S(1)} %copy.48.part_ref, bf16[8,192,2048]{2,1,0:T(8,128)(2,1)S(1)} %bitcast.52), custom_call_target="tpu_custom_call" | custom-call | tf_op jit(solution)/shard_map/factors/pallas_call | solution.py:125
  237.5 2.6 reshape.25
  240.1 0.0 copy-start.1
  240.1 1.6 convert_multiply_fusion
  241.7 0.8 copy-done.1
  242.5 10.2 %convolution_bitcast_fusion = f32[8,32,1792]{2,1,0:T(8,128)} fusion(bf16[8,4,128,1792,1]{3,2,1,0,4:T(8,128)(2,1)} %bitcast.61, bf16[4,8,32,8,24]{4,3,2,1,0:T(8,128)(2,1)S(1)} %copy-done.1, f32[8,8,4,128]{3,2,1,0:T(4,128)S(1)} %copy.39, f32[4,8,8,128]{3,0,1,2:T(4,128)S(1)} %copy.31), kind=kOutput, calls=%fused_computation.7 | convolution fusion | flops 3811311616 | bytes 17170432 | tf_op jit(solution)/shard_map/jrbpt,bptd->jrd/dot_general | solution.py:193
  (5 shorter events, 0.1 us)
Async XLA Ops:
  7.2 136.8 %all-gather.4.cloned.1.call-start = ((), (), s32[]{:S(2)}) async-start(), calls=%async_computation.1 | async-start | bytes 16515072 | tf_op jit(solution)/shard_map/all_gather | solution.py:154
  60.0 2.5 copy-start.2
  60.0 2.5 copy-start.3
  153.3 2.8 %copy-start = (bf16[1,8,192,2048]{3,2,1,0:T(8,128)(2,1)S(1)}, bf16[1,8,192,2048]{3,2,1,0:T(8,128)(2,1)}, u32[]{:S(2)}) copy-start(bf16[1,8,192,2048]{3,2,1,0:T(8,128)(2,1)} %param.8) | copy-start | bytes 18874372
  240.1 2.3 copy-start.1
Sparse Core Ops, SparseCore 0:
  62.6 81.3 all-gather.3

commit v3 on v2

--- a/solution.py
+++ b/solution.py
@@ -146,12 +146,134 @@
     )(part, hidden)
 
 
+def gather_kernel(
+    n_expert, n_dp, x_ref, all_ref,
+    own_sem, z_send, z_recv, one_send, one_recv, two_send, two_recv, core_send, core_recv,
+):
+    me, z = lax.axis_index("expert"), lax.axis_index("dp")
+    chips = n_expert // 2
+    wide = math.isqrt(chips)
+    sides = (wide, chips // wide)
+    core, chip = lax.rem(me, 2), me // 2
+    spot = (lax.rem(chip, wide), chip // wide)
+    half, cols = x_ref.shape[0] // 2, all_ref.shape[3]
+
+    def shifted(dim, by):
+        return lax.rem(spot[dim] + by + sides[dim], sides[dim])
+
+    def block(x, y, c):
+        return (y * wide + x) * 2 + c
+
+    def neighbour(dim, by):
+        moved = shifted(dim, by)
+        return block(moved, spot[1], core) if dim == 0 else block(spot[0], moved, core)
+
+    def source(dim, first, second, c):
+        x, y = (first, second) if dim == 0 else (second, first)
+        return block(shifted(0, -x), shifted(1, -y), c)
+
+    barrier = pltpu.get_barrier_semaphore()
+    greeted = [{"dp": lax.rem(z + k, n_dp)} for k in range(1, n_dp)]
+    greeted += [{"expert": neighbour(d, by)} for d in range(2) for by in range(1, sides[d])]
+    greeted += [{"expert": block(spot[0], spot[1], 1 - core)}]
+    for peer in greeted:
+        pl.semaphore_signal(barrier, inc=1, device_id=peer, device_id_type=MESH)
+    pl.semaphore_wait(barrier, len(greeted))
+
+    sent = []
+
+    def push(src, dst, send_sem, recv_sem, device):
+        copy = pltpu.make_async_remote_copy(
+            src_ref=src, dst_ref=dst, send_sem=send_sem, recv_sem=recv_sem,
+            device_id=device, device_id_type=MESH,
+        )
+        copy.start()
+        sent.append(copy)
+        return copy
+
+    def columns(r):
+        return x_ref.at[:, pl.ds(pl.multiple_of(r * cols, 128), cols)]
+
+    own = pltpu.make_async_copy(columns(z), all_ref.at[me, z], own_sem)
+    own.start()
+    arrive_z, arrive_one, arrive_two, arrive_core = {}, {}, {}, []
+    for k in range(1, n_dp):
+        to = lax.rem(z + k, n_dp)
+        arrive_z[k] = push(
+            columns(to), all_ref.at[me, z], z_send.at[k - 1], z_recv.at[k - 1], {"dp": to}
+        )
+
+    def rows(b, k, h):
+        return all_ref.at[b, lax.rem(z - k + n_dp, n_dp), pl.ds(h * half, half)]
+
+    def swap(k, h, first, second):
+        part = rows(source(h, first, second, core), k, h)
+        at = (h, k, first, second)
+        partner = {"expert": block(spot[0], spot[1], 1 - core)}
+        arrive_core.append(push(part, part, core_send.at[at], core_recv.at[at], partner))
+
+    def onward(k, h, first):
+        part = rows(source(h, first, 0, core), k, h)
+        for by in range(1, sides[1 - h]):
+            at = (h, k, first, by - 1)
+            arrive_two[at] = push(
+                part, part, two_send.at[at], two_recv.at[at], {"expert": neighbour(1 - h, by)}
+            )
+        swap(k, h, first, 0)
+
+    for k in range(n_dp + 2):
+        if k < n_dp:
+            if k:
+                arrive_z[k].wait_recv()
+            else:
+                own.wait()
+            for h in range(2):
+                part = rows(me, k, h)
+                for by in range(1, sides[h]):
+                    at = (h, k, by - 1)
+                    arrive_one[at] = push(
+                        part, part, one_send.at[at], one_recv.at[at], {"expert": neighbour(h, by)}
+                    )
+            for h in range(2):
+                onward(k, h, 0)
+        if 0 <= k - 1 < n_dp:
+            for h in range(2):
+                for by in range(1, sides[h]):
+                    arrive_one[(h, k - 1, by - 1)].wait_recv()
+                    onward(k - 1, h, by)
+        if 0 <= k - 2 < n_dp:
+            for h in range(2):
+                for first in range(sides[h]):
+                    for by in range(1, sides[1 - h]):
+                        arrive_two[(h, k - 2, first, by - 1)].wait_recv()
+                        swap(k - 2, h, first, by)
+    for copy in arrive_core:
+        copy.wait_recv()
+    for copy in sent:
+        copy.wait_send()
+
+
 def gathered(grads):
-    n_dp = lax.axis_size("dp")
+    n_expert, n_dp = lax.axis_size("expert"), lax.axis_size("dp")
     tokens, width = grads.shape
-    split = grads.reshape(tokens, n_dp, width // n_dp).transpose(1, 0, 2)
-    split = lax.all_to_all(split, "dp", split_axis=0, concat_axis=0, tiled=True)
-    return lax.all_gather(split, "expert", axis=0)
+    long = max(math.isqrt(n_expert // 2), n_expert // 2 // math.isqrt(n_expert // 2))
+    dma = pltpu.SemaphoreType.DMA
+    return pl.pallas_call(
+        functools.partial(gather_kernel, n_expert, n_dp),
+        out_shape=jax.ShapeDtypeStruct((n_expert, n_dp, tokens, width // n_dp), grads.dtype),
+        in_specs=[pl.BlockSpec(memory_space=pltpu.VMEM)],
+        out_specs=pl.BlockSpec(memory_space=pl.ANY),
+        scratch_shapes=[
+            dma(()), dma((n_dp - 1,)), dma((n_dp - 1,)),
+            dma((2, n_dp, long)), dma((2, n_dp, long)),
+            dma((2, n_dp, long, long)), dma((2, n_dp, long, long)),
+            dma((2, n_dp, long, long)), dma((2, n_dp, long, long)),
+        ],
+        compiler_params=pltpu.CompilerParams(
+            collective_id=1, has_side_effects=True, vmem_limit_bytes=56 * 2**20
+        ),
+        name="gather_rows",
+    )(grads)
 
 
 def local(out_grads, expert_ids, gate_probs, hidden_acts, q_previous):

time: 261 us -> 239 us (0.916)
  Pallas kernels: 81.4 us -> 161 us
  blocking collectives: 90 us -> 43.9 us
  waiting for transfers between devices: 39.5 us -> 0 us
  between operations: 14.2 us -> 0.72 us
  local copies, waits for them, and re-layouts: 13.5 us -> 6.39 us
    pallas_call x0 -> x1, Pallas kernels: none -> 71.5 us  [gathered(): pl.pallas_call(functools.partial(gather_kernel, n_expert, n_dp), out_shap...]
    all_to_all x1 -> x0, blocking collectives: 48.9 us -> none  [gathered(): split = lax.all_to_all(split, 'dp', split_axis=0, concat_axis=0, tiled=True)]
    all_gather x1 -> x0, waiting for transfers between devices: 39.5 us -> none  [gathered(): return lax.all_gather(split, 'expert', axis=0)]
    pallas_call x1, Pallas kernels: 81.4 us -> 89.5 us  [factors(): pl.pallas_call(functools.partial(factor_kernel, n), out_shape=(jax.ShapeD...]
    unnamed x10 -> x3, local copies, waits for them, and re-layouts: 7.5 us -> 2.83 us
    all_gather x1, blocking collectives: 41.1 us -> 43.9 us  [local(): route = lax.all_gather(route, ('dp', 'expert'), axis=0)]
  transfers between devices with their start and end apart: 1 -> 0, of which waited for: 1 -> 0; matrix products, arithmetic and copies ran while one was open for 0% -> 0% of each run, Pallas kernels for 0% -> 0%
where the time goes in v3:
time: 239 us; the launch traced here: 235 us
  Pallas kernels  161 us (67%)
  blocking collectives  43.9 us (18%)
  matrix products  19.6 us (8%)
  local copies, waits for them, and re-layouts  6.39 us (3%)
  other arithmetic  3.34 us (1%)
    pallas_call x1, Pallas kernels, factors(): pl.pallas_call(functools.partial(factor_kernel, n), out_shape=(jax.ShapeD...  89.5 us
    pallas_call x1, Pallas kernels, gathered(): pl.pallas_call(functools.partial(gather_kernel, n_expert, n_dp), out_shap...  71.5 us
    all_gather x1, blocking collectives, local(): route = lax.all_gather(route, ('dp', 'expert'), axis=0)  43.9 us
    dot_general x1, matrix products, local(): jnp.einsum('jrbpt,bptd->jrd', spread, grads, preferred_element_type=F32)  10.8 us
    dot_general x1, matrix products, local(): jnp.einsum('jrbpt,pbjct->pjrbc', mixed, pick, preferred_element_type=F32)  8.59 us

profile of v3, /device:TPU:0, one launch (start us, length us, event | category | flops | bytes accessed | tf_op | source)
XLA Modules:
  0.0 235.0 jit_solution(11079083875436928144)
XLA Ops:
  0.6 0.7 convert_bitcast_fusion
  1.3 0.7 pad_maximum_fusion
  2.0 43.9 %all-gather = f32[4096,16]{0,1:T(8,128)S(1)} all-gather(f32[128,16]{0,1:T(8,128)S(1)} %pad_maximum_fusion), channel_id=2, replica_groups=mesh['expert'=8,'dp'=4] {'dp','expert'}, dimensions={0}, use_global_device_ids=true | all-gather | bytes 270336 | tf_op jit(solution)/shard_map/all_gather | solution.py:291
  45.9 0.1 copy.29
  46.0 0.2 fusion.18
  46.3 0.2 compare_reduce_fusion
  46.5 0.2 convolution_select_fusion
  46.6 0.1 copy.13
  46.7 71.5 %gather_rows.1 = bf16[8,4,128,1792]{3,2,1,0:T(8,128)(2,1)} custom-call(bf16[128,7168]{1,0:T(8,128)(2,1)} %bitcast.54), custom_call_target="tpu_custom_call" | custom-call | tf_op jit(solution)/shard_map/gather_rows/pallas_call | solution.py:261
  118.3 8.6 %fusion.7 = bf16[4,8,8,24,32]{4,3,2,1,0:T(8,128)(2,1)S(1)} fusion(f32[8,8,4,128]{3,1,0,2:T(8,128)S(1)} %copy.15, bf16[8,32,7168]{2,1,0:T(8,128)(2,1)} %param.9, s32[]{:T(128)S(6)} %select_n.12, bf16[8,4,128,1792]{3,2,1,0:T(8,128)(2,1)} %gather_rows.1, f32[4,8,8,128]{3,0,1,2:T(4,128)S(1)} %copy.13), kind=kOutput, calls=%fused_computation.12 | convolution fusion | flops 3811508224 | bytes 16252932 | tf_op jit(solution)/shard_map/jrbpt,pbjct->pjrbc/dot_general | solution.py:309
  126.9 0.8 copy.28.part_ref
  127.6 0.0 copy-start
  127.7 2.8 %copy-done = bf16[1,8,192,2048]{3,2,1,0:T(8,128)(2,1)S(1)} copy-done((bf16[1,8,192,2048]{3,2,1,0:T(8,128)(2,1)S(1)}, bf16[1,8,192,2048]{3,2,1,0:T(8,128)(2,1)}, u32[]{:S(2)}) %copy-start) | copy-done | bytes 6291480
  130.4 89.5 %factors.1 = (bf16[8,32,2048]{2,1,0:T(8,128)(2,1)S(1)}, bf16[4,8,32,192]{3,2,1,0:T(8,128)(2,1)S(1)}) custom-call(bf16[4,8,32,192]{3,2,1,0:T(8,128)(2,1)S(1)} %copy.28.part_ref, bf16[8,192,2048]{2,1,0:T(8,128)(2,1)S(1)} %bitcast.53), custom_call_target="tpu_custom_call" | custom-call | tf_op jit(solution)/shard_map/factors/pallas_call | solution.py:125
  220.0 2.6 %reshape.25 = bf16[4,8,32,8,24]{4,3,2,1,0:T(8,128)(2,1)} reshape(bf16[4,8,32,192]{3,2,1,0:T(8,128)(2,1)S(1)} %get-tuple-element.5) | data formatting | bytes 786432 | tf_op jit(solution)/shard_map/reshape | solution.py:312
  222.5 0.1 copy.19
  222.6 10.8 %convolution_bitcast_fusion = f32[8,32,1792]{2,1,0:T(8,128)} fusion(bf16[4,8,32,8,24]{4,3,2,1,0:T(8,128)(2,1)} %reshape.25, f32[8,8,4,128]{3,2,1,0:T(4,128)S(1)} %copy.19, bf16[8,4,128,1792]{3,2,1,0:T(8,128)(2,1)} %gather_rows.1, f32[4,8,8,128]{3,0,1,2:T(4,128)S(1)} %copy.13), kind=kOutput, calls=%fused_computation.7 | convolution fusion | flops 3811311616 | bytes 17170432 | tf_op jit(solution)/shard_map/jrbpt,bptd->jrd/dot_general | solution.py:315
  233.5 1.6 convert_multiply_fusion
  (3 shorter events, 0.1 us)
Async XLA Ops:
  127.6 2.8 %copy-start = (bf16[1,8,192,2048]{3,2,1,0:T(8,128)(2,1)S(1)}, bf16[1,8,192,2048]{3,2,1,0:T(8,128)(2,1)}, u32[]{:S(2)}) copy-start(bf16[1,8,192,2048]{3,2,1,0:T(8,128)(2,1)} %param.8) | copy-start | bytes 18874372
